TPU v7x, 32 devices: a whole 2x2x4 slice. The times are simulated.
32 devices in a mesh: context: 2 (over core), tensor: 4 (over y, x), fsdp: 4 (over z).
Axes of the slice: x: 2, y: 2, z: 4, core: 2. Of those that a mesh axis runs over, the one named last changes fastest.
Arguments:
- input_raw: bfloat16 [4, 1024, 5120], P('fsdp', ('context', 'tensor')), may hold values from -6 to 6
- state_proj_raw: bfloat16 [4, 1024, 256], P('fsdp', ('context', 'tensor')), may hold values from -6 to 6
- gate_branch: bfloat16 [4, 1024, 5120], P('fsdp', ('context', 'tensor')), may hold values from -6 to 6
- step_raw: bfloat16 [4, 1024, 80], P('fsdp', ('context', 'tensor')), may hold values from -6 to 6
- convolution_taps: float32 [4, 5376], replicated, may hold values from -3 to 3
- convolution_bias: float32 [5376], replicated, may hold values from -3 to 3
- step_bias: float32 [80], P('tensor'), may hold values from -1.5 to 0.5
- decay_log_rate: float32 [80], P('tensor'), may hold values from -13 to -2, as said below
- skip_weight: float32 [80], P('tensor'), may hold values from 0.5 to 2
- gated_norm_gain: float32 [5120], P('tensor'), may hold values from 0.1 to 1.9
- output_weight: bfloat16 [5120, 2560], P('tensor', 'fsdp'), may hold values from -0.078125 to 0.078125
- adapter_down: bfloat16 [5120, 16], P('tensor'), may hold values from -0.078125 to 0.078125
- adapter_up: bfloat16 [16, 2560], replicated, may hold values from -0.29882812 to 0.29882812
- cotangent: bfloat16 [4, 1024, 2560], P('fsdp', ('context', 'tensor')), may hold values from -6 to 6
Outputs:
- mixed: bfloat16 [4, 1024, 2560], P('fsdp', ('context', 'tensor'))
- grad_a: float32 [5120, 16], P('tensor')
- grad_b: float32 [16, 2560], replicated
Inputs may be any that keep to these rules, and one draw needn't show every extreme that they name: `decay_log_rate`: logarithms of positive decay rates.
All inputs are finite; a program needn't handle non-finite values.
Results may differ from a plain program's by a relative error of at most 0.017.
Values may be sent and summed in bfloat16 or wider, within the bound.
No kernel may reach another device: no remote copies, remote signals or barrier semaphores. Data moves between devices by JAX's collectives and lax.ppermute only.
A program may use at most 128 MiB of HBM per device.

v0:
```python
import math
import jax
import jax.numpy as jnp
from jax import lax
from jax.sharding import PartitionSpec as P

epsilon = 1e-05


def passed_along(value, axis, steps):
    count = lax.axis_size(axis)
    leading, last = (max(0, -steps), min(count, count - steps))
    return lax.ppermute(value, axis, [(source, source + steps) for source in range(leading, last)])


def entering(value, axis, join, neutral):
    count, mine = (lax.axis_size(axis), lax.axis_index(axis))
    pieces = jax.tree.map(lambda part: lax.all_gather(part, axis), value)
    subtotal = jax.tree.map(
        lambda part, zero: jnp.full_like(part, 0) + jnp.asarray(zero, part.dtype), value, neutral
    )

    def lap(position, subtotal):
        longer = join(subtotal, jax.tree.map(lambda part: part[position], pieces))
        return jax.tree.map(lambda new, old: jnp.where(position < mine, new, old), longer, subtotal)

    return lax.fori_loop(0, count - 1, lap, subtotal)


def convolve(values, before, weight, bias_row):
    length = values.shape[0]
    extended = jnp.concatenate([before, values], axis=0)
    pre_act = bias_row[None, :] + weight[0][None, :] * extended[0:length].astype(jnp.float32)
    for tap_index in range(1, weight.shape[0]):
        pre_act = pre_act + weight[tap_index][None, :] * extended[
            tap_index : tap_index + length
        ].astype(jnp.float32)
    return jax.nn.silu(pre_act).astype(jnp.bfloat16)


def ssd_blocks(x_heads, b_rows, c_rows, step_size, log_decay, block_len):
    highest = lax.Precision.HIGHEST
    length = x_heads.shape[0]
    head_count = x_heads.shape[1]
    head_size = x_heads.shape[2]
    state_size = b_rows.shape[1]
    blocks = length // block_len
    causal = jnp.arange(block_len)[:, None] >= jnp.arange(block_len)[None, :]

    def advance(state_now, pieces):
        x_block, b_block, c_block, step_block, decay_block = pieces
        cum_decay = jnp.cumsum(decay_block, axis=0)
        cum_heads = cum_decay.T
        gap_decay = cum_heads[:, :, None] - cum_heads[:, None, :]
        decay_mat = jnp.where(causal[None], jnp.exp(jnp.where(causal[None], gap_decay, 0.0)), 0.0)
        gram_mat = jnp.dot(c_block, b_block.T, precision=highest)
        x_scaled = x_block * step_block[:, :, None]
        y_inner = jnp.einsum(
            "hij,jhp->ihp", decay_mat * gram_mat[None], x_scaled, precision=highest
        )
        y_state = jnp.exp(cum_decay)[:, :, None] * jnp.einsum(
            "in,hpn->ihp", c_block, state_now, precision=highest
        )
        tail_decay = jnp.exp(cum_decay[-1][None, :] - cum_decay)
        state_next = jnp.exp(cum_decay[-1])[:, None, None] * state_now + jnp.einsum(
            "jhp,jn->hpn", x_scaled * tail_decay[:, :, None], b_block, precision=highest
        )
        return (state_next, y_inner + y_state)

    start_state = jnp.zeros((head_count, head_size, state_size), jnp.float32)
    state_end, y_blocks = lax.scan(
        advance,
        start_state,
        (
            x_heads.reshape(blocks, block_len, head_count, head_size),
            b_rows.reshape(blocks, block_len, state_size),
            c_rows.reshape(blocks, block_len, state_size),
            step_size.reshape(blocks, block_len, head_count),
            log_decay.reshape(blocks, block_len, head_count),
        ),
    )
    return (y_blocks.reshape(length, head_count, head_size), state_end)


def chain_states(earlier, later):
    return (earlier[0] + later[0], jnp.exp(later[0])[:, None, None] * earlier[1] + later[1])


def row_slice(values, start_row, row_count):
    return lax.dynamic_slice_in_dim(values, start_row, row_count, 0)


def shards(
    input_raw,
    state_proj_raw,
    gate_branch,
    step_raw,
    convolution_taps,
    convolution_bias,
    step_bias,
    decay_log_rate,
    skip_weight,
    gated_norm_gain,
    output_weight,
    adapter_down,
    adapter_up,
    cotangent,
):
    highest = lax.Precision.HIGHEST
    tok_rows = input_raw.shape[1]
    inner_width = input_raw.shape[2]
    state_size = state_proj_raw.shape[2] // 2
    rim_width = convolution_taps.shape[0] - 1
    joined = jnp.concatenate([input_raw[0], state_proj_raw[0]], axis=1)
    before = passed_along(joined[tok_rows - rim_width :], ("context", "tensor"), 1)
    convolved = convolve(joined, before, convolution_taps, convolution_bias)
    x_heads_raw, z_heads, dt_heads = (
        lax.all_to_all(
            convolved[:, :inner_width], "tensor", split_axis=1, concat_axis=0, tiled=True
        ),
        lax.all_to_all(gate_branch[0], "tensor", split_axis=1, concat_axis=0, tiled=True),
        lax.all_to_all(step_raw[0], "tensor", split_axis=1, concat_axis=0, tiled=True),
    )
    shared = lax.all_gather(convolved[:, inner_width:], "tensor", axis=0, tiled=True)
    span_rows = x_heads_raw.shape[0]
    local_heads = dt_heads.shape[1]
    local_width = x_heads_raw.shape[1]
    head_size = local_width // local_heads
    x_heads = x_heads_raw.astype(jnp.float32).reshape(span_rows, local_heads, head_size)
    b_rows = shared[:, :state_size].astype(jnp.float32)
    c_rows = shared[:, state_size:].astype(jnp.float32)
    step_size = jax.nn.softplus(dt_heads.astype(jnp.float32) + step_bias[None, :])
    log_decay = -step_size * jnp.exp(decay_log_rate)[None, :]
    y_local, state_end = ssd_blocks(
        x_heads, b_rows, c_rows, step_size, log_decay, math.gcd(span_rows, 256)
    )
    log_total = jnp.sum(log_decay, axis=0)
    prior_total, incoming = entering(
        (log_total, state_end),
        "context",
        chain_states,
        (jnp.zeros_like(log_total), jnp.zeros_like(state_end)),
    )
    reach_decay = jnp.exp(jnp.cumsum(log_decay, axis=0))
    y_heads = y_local + reach_decay[:, :, None] * jnp.einsum(
        "tn,hpn->thp", c_rows, incoming, precision=highest
    )
    y_heads = y_heads + skip_weight[None, :, None] * x_heads
    gated = y_heads.reshape(span_rows, local_width) * jax.nn.silu(z_heads.astype(jnp.float32))
    squares = jnp.sum(gated * gated, axis=1)
    gated_output = (gated * gated_norm_gain[None, :]).astype(jnp.bfloat16)
    adapter_piece = jnp.dot(gated_output, adapter_down, preferred_element_type=jnp.float32)
    full_width = local_width * lax.axis_size("tensor")
    columns = lax.all_gather(output_weight, "fsdp", axis=1, tiled=True)
    own_start = lax.axis_index("tensor") * tok_rows
    sum_squares, adapter_all = (
        lax.psum(squares.astype(jnp.bfloat16), "tensor").astype(jnp.float32),
        lax.psum(adapter_piece.astype(jnp.bfloat16), "tensor").astype(jnp.float32),
    )
    scale_all = lax.rsqrt(sum_squares / full_width + epsilon)
    adapter_all = adapter_all.astype(jnp.bfloat16)
    leader = (lax.axis_index("tensor") == 0).astype(jnp.float32)
    start_row = jnp.int32(0)
    frozen_piece = jnp.dot(
        row_slice(gated_output, start_row, lax.axis_size("tensor") * tok_rows),
        columns,
        preferred_element_type=jnp.float32,
    )
    frozen_piece = frozen_piece + 2.0 * leader * jnp.dot(
        row_slice(adapter_all, start_row, lax.axis_size("tensor") * tok_rows),
        adapter_up,
        preferred_element_type=jnp.float32,
    )
    summed = lax.psum_scatter(
        (
            row_slice(scale_all, start_row, lax.axis_size("tensor") * tok_rows)[:, None]
            * frozen_piece
        ).astype(jnp.bfloat16),
        "tensor",
        scatter_dimension=0,
        tiled=True,
    )
    row_norm_scale = row_slice(scale_all, own_start, tok_rows)
    adapter_branch = row_slice(adapter_all, own_start, tok_rows)
    cotangent_rows = cotangent[0]
    token_total = (
        tok_rows * lax.axis_size("context") * lax.axis_size("tensor") * lax.axis_size("fsdp")
    )
    lowrank_factor = 2.0 / math.sqrt(token_total)
    weighted = lowrank_factor * row_norm_scale[:, None] * adapter_branch.astype(jnp.float32)
    grad_b_local = jnp.dot(weighted.T, cotangent_rows.astype(jnp.float32), precision=highest)
    adapter_gradient = (
        lowrank_factor
        * row_norm_scale[:, None]
        * jnp.dot(cotangent_rows, adapter_up.T, preferred_element_type=jnp.float32)
    )
    adapter_span = lax.all_gather(adapter_gradient, "tensor", axis=0, tiled=True)
    grad_a_local = jnp.dot(gated_output.astype(jnp.float32).T, adapter_span, precision=highest)
    grad_a, grad_b_part = lax.psum((grad_a_local, grad_b_local), ("context", "fsdp"))
    grad_b = lax.psum(grad_b_part.astype(jnp.bfloat16), "tensor").astype(jnp.float32)
    return (summed[None], grad_a, grad_b)


def solution(mesh):
    placed = (
        P("fsdp", ("context", "tensor"), None),
        P("fsdp", ("context", "tensor"), None),
        P("fsdp", ("context", "tensor"), None),
        P("fsdp", ("context", "tensor"), None),
        P(),
        P(),
        P("tensor"),
        P("tensor"),
        P("tensor"),
        P("tensor"),
        P("tensor", "fsdp"),
        P("tensor", None),
        P(),
        P("fsdp", ("context", "tensor"), None),
    )
    return jax.shard_map(
        shards,
        mesh=mesh,
        in_specs=placed,
        out_specs=(P("fsdp", ("context", "tensor"), None), P("tensor", None), P()),
        check_vma=False,
    )
```

profile of v0, /device:TPU:0, one launch (start us, length us, event | category | flops | bytes accessed | tf_op | source)
XLA Modules:
  0.0 443.3 jit_solution(7496762377417726398)
XLA Ops:
  8.3 4.9 %collective-permute-start = (bf16[3,5376]{1,0:T(4,128)(2,1)S(1)}, bf16[3,5376]{1,0:T(4,128)(2,1)S(1)}, u32[]{:S(2)}, u32[]{:S(2)}) collective-permute-start(bf16[3,5376]{1,0:T(4,128)(2,1)S(1)} %fusion.75), channel_id=1, source_target_pairs={{0,4},{4,8},{8,12},{12,16},{16,20},{20,24},{24,28},{1,5},{5,9},{9,... | collective-permute-start | bytes 96776 | tf_op jit(solution)/shard_map/ppermute | solution.py:13
  24.6 4.2 all-to-all-start.1
  30.3 19.2 %all_gather.21 = bf16[512,256]{1,0:T(8,128)(2,1)S(1)} all-gather(bf16[128,256]{1,0:T(8,128)(2,1)S(1)} %slice.84), channel_id=1, replica_groups=mesh['context'=2,'tensor'=4,'fsdp'=4] {'tensor'}, dimensions={0}, use_global_device_ids=true | all-gather | bytes 327680 | tf_op jit(solution)/shard_map/all_gather | solution.py:124
  51.1 5.4 %copy.68 = f32[4,128,1280]{1,0,2:T(4,128)S(1)} copy(f32[4,128,1280]{1,2,0:T(8,128)S(1)} %convert_bitcast_fusion.1) | data formatting | bytes 5242880 | tf_op jit(solution)/shard_map/convert_element_type | solution.py:129
  59.9 93.5 %while.4 = (s32[]{:T(128)}, f32[20,64,128]{2,1,0:T(8,128)}, f32[2,256,20,64]{1,0,3,2:T(2,128)}, f32[2,256,20]{1,0,2:T(2,128)}, f32[2,256,20,64]{1,0,3,2:T(2,128)...) while((s32[]{:T(128)}, f32[20,64,128]{2,1,0:T(8,128)}, ...), condition=%wide.region_3.4_spmd.clone.clone, body=%wide.region_0.3_spmd.clone.clone.sunk | while | flops 2122191872 | bytes 18280176 | solution.py:71
  66.2 6.0 %fusion.115 = f32[256,20,64]{0,2,1:T(8,128)S(1)} fusion(f32[256,256]{1,0:T(8,128)S(1)} %fusion.114, f32[20,256]{1,0:T(8,128)S(1)} %bitcast.176, pred[256,256]{1,0:T(8,128)(4,1)S(1)} %iota_compare_fusion.2, f32[1,256,20,64]{1,0,3,2:T(1,128)S(1)} %constant_dynamic-slice_fusion.5, f32[256,20]{0,1:T(8,128)S(1)} %bitcast.180), kind=kOutput, calls=%fused_computation.15.clone.1 | convolution fusion | flops 1012203520 | bytes 2990080 | tf_op jit(solution)/shard_map/while/body/eval_jaxpr/hij,jhp->ihp/dot_general | solution.py:58
  76.5 27.0 %dynamic_update_slice.7 = f32[2,256,20,64]{1,0,3,2:T(2,128)} dynamic-update-slice(f32[2,256,20,64]{1,0,3,2:T(2,128)} %get-tuple-element.267, f32[1,256,20,64]{1,0,3,2:T(1,128)S(1)} %copy.124, s32[]{:T(128)} %get-tuple-element.265, s32[]{:T(128)} %constant.41.clone.1..sunk, s32[]{:T(128)} %constant.41.clone.1..sunk, s32[]{:T(128)} %constant.41.clone.1..sunk) | dynamic-update-slice | bytes 2621444 | tf_op jit(solution)/shard_map/while/body/jit(dynamic_update_index_in_dim)/dynamic_update_slice | solution.py:71
  112.7 6.0 %fusion.115 = f32[256,20,64]{0,2,1:T(8,128)S(1)} fusion(f32[256,256]{1,0:T(8,128)S(1)} %fusion.114, f32[20,256]{1,0:T(8,128)S(1)} %bitcast.176, pred[256,256]{1,0:T(8,128)(4,1)S(1)} %iota_compare_fusion.2, f32[1,256,20,64]{1,0,3,2:T(1,128)S(1)} %constant_dynamic-slice_fusion.5, f32[256,20]{0,1:T(8,128)S(1)} %bitcast.180), kind=kOutput, calls=%fused_computation.15.clone.1 | convolution fusion | flops 1012203520 | bytes 2990080 | tf_op jit(solution)/shard_map/while/body/eval_jaxpr/hij,jhp->ihp/dot_general | solution.py:58
  123.3 27.0 %dynamic_update_slice.7 = f32[2,256,20,64]{1,0,3,2:T(2,128)} dynamic-update-slice(f32[2,256,20,64]{1,0,3,2:T(2,128)} %get-tuple-element.267, f32[1,256,20,64]{1,0,3,2:T(1,128)S(1)} %copy.124, s32[]{:T(128)} %get-tuple-element.265, s32[]{:T(128)} %constant.41.clone.1..sunk, s32[]{:T(128)} %constant.41.clone.1..sunk, s32[]{:T(128)} %constant.41.clone.1..sunk) | dynamic-update-slice | bytes 2621444 | tf_op jit(solution)/shard_map/while/body/jit(dynamic_update_index_in_dim)/dynamic_update_slice | solution.py:71
  156.2 3.5 all-to-all-start.2
  166.6 6.9 %all-to-all-done.2 = bf16[128,4,1280]{0,2,1:T(8,128)(2,1)S(1)} async-done(((bf16[128,4,1280]{0,2,1:T(8,128)(2,1)}), bf16[128,4,1280]{0,2,1:T(8,128)(2,1)S(1)}, u32[]{:S(2)}, u32[]{:S(2)}) %all-to-all-start.2) | async-done | bytes 1310752 | tf_op jit(solution)/shard_map/all_to_all | solution.py:121
  176.1 4.3 copy.79
  180.4 4.3 reshape.166
  186.8 4.9 %reshape.152 = f32[512,20,64]{0,2,1:T(8,128)} reshape(f32[2,256,20,64]{1,0,3,2:T(2,128)} %get-tuple-element.72) | data formatting | bytes 5242880 | tf_op jit(solution)/shard_map/reshape | solution.py:82
  191.8 6.3 %multiply_reduce_fusion = (bf16[512]{0:T(512)(128)(2,1)S(1)}, f32[512,20,64]{0,2,1:T(8,128)}) fusion(f32[512,20,64]{0,2,1:T(8,128)S(1)} %copy-done.6, f32[512,20,64]{0,2,1:T(8,128)} %reshape.165, f32[20]{0:T(128)S(1)} %copy-done.22, f32[512,20,64]{0,2,1:T(8,128)} %reshape.152, f32[40,64,128]{2,1,0:T(8,128)} %all-gather.7.cloned.1.call-done, ...), kind=kOutput, calls=%fused_computation.66 | convolution fusion | flops 1014169088 | bytes 11323393 | tf_op jit(solution)/shard_map/tn,hpn->thp/dot_general | solution.py:145
  198.1 3.4 copy.80
  204.7 15.3 %all-reduce.1 = (bf16[512,16]{0,1:T(8,128)(2,1)S(1)}, bf16[512]{0:T(512)(128)(2,1)S(1)}) all-reduce(bf16[512,16]{0,1:T(8,128)(2,1)S(1)} %convolution_convert_fusion, bf16[512]{0:T(512)(128)(2,1)S(1)} %get-tuple-element.195), channel_id=1, replica_groups=mesh['context'=2,'tensor'=4,'fsdp'=4] {'tensor'}, use_global_device_ids=true, to_apply=%region_9.10 | all-reduce | flops 8704 | bytes 34816 | tf_op jit(solution)/shard_map/psum | solution.py:158
  220.6 8.2 %all_gather.27 = f32[512,16]{0,1:T(8,128)S(1)} all-gather(f32[128,16]{0,1:T(8,128)S(1)} %convolution_multiply_fusion.1), channel_id=1, replica_groups=mesh['context'=2,'tensor'=4,'fsdp'=4] {'tensor'}, dimensions={0}, use_global_device_ids=true | all-gather | bytes 40960 | tf_op jit(solution)/shard_map/all_gather | solution.py:197
  228.8 51.7 %all-reduce.9 = bf16[16,2560]{1,0:T(8,128)(2,1)} all-reduce(f32[16,2560]{1,0:T(8,128)S(1)} %fusion.55), channel_id=1, replica_groups=mesh['context'=2,'tensor'=4,'fsdp'=4] {'context','fsdp'}, use_global_device_ids=true, to_apply=%region_12.13 | all-reduce | flops 40960 | bytes 245760 | tf_op jit(solution)/shard_map/psum | solution.py:199
  282.0 9.7 %all-gather.5.cloned.1.call-done = bf16[1280,2560]{1,0:T(8,128)(2,1)} async-done(((bf16[1280,640]{1,0:T(8,128)(2,1)}), bf16[1280,2560]{1,0:T(8,128)(2,1)}) %all-gather.5.cloned.1.call-update) | async-done | bytes 6553616 | tf_op jit(solution)/shard_map/all_gather | solution.py:154
  291.6 5.7 %fusion.84 = f32[512,2560]{1,0:T(8,128)S(1)} fusion(bf16[512,1280]{1,0:T(8,128)(2,1)S(1)} %fusion.52, bf16[1280,2560]{1,0:T(8,128)(2,1)} %all-gather.5.cloned.1.call-done), kind=kOutput, calls=%fused_computation.121 | convolution fusion | flops 3355443200 | bytes 13107200 | tf_op jit(solution)/shard_map/dot_general | solution.py:164
  299.8 35.1 %all-reduce.8.cloned.1.call-done = bf16[16,2560]{1,0:T(8,128)(2,1)} async-done(((bf16[16,2560]{1,0:T(8,128)(2,1)}), bf16[16,2560]{1,0:T(8,128)(2,1)}) %all-reduce.8.cloned.1.call-update) | async-done | bytes 81936 | tf_op jit(solution)/shard_map/psum | solution.py:200
  336.4 52.5 %all-reduce.6.cloned.1.call-done = f32[1280,16]{0,1:T(8,128)} async-done(((f32[1280,16]{0,1:T(8,128)}), f32[1280,16]{0,1:T(8,128)}) %all-reduce.6.cloned.1.call-update) | async-done | bytes 81936 | tf_op jit(solution)/shard_map/psum | solution.py:199
  388.9 46.4 %reduce-scatter.2.cloned.1.call-done = bf16[128,2560]{1,0:T(8,128)(2,1)} async-done(((bf16[512,2560]{1,0:T(8,128)(2,1)}), bf16[128,2560]{1,0:T(8,128)(2,1)}) %reduce-scatter.2.cloned.1.call-update) | async-done | bytes 655376 | tf_op jit(solution)/shard_map/reduce_scatter | solution.py:174
  (163 shorter events, 70.5 us)
Async XLA Ops:
  7.2 212.8 %copy-start = (bf16[1,128,2560]{2,1,0:T(8,128)(2,1)S(1)}, bf16[1,128,2560]{2,1,0:T(8,128)(2,1)}, u32[]{:S(2)}) copy-start(bf16[1,128,2560]{2,1,0:T(8,128)(2,1)} %param.29) | copy-start | bytes 1966084
  7.2 13.6 %copy-start.5 = (bf16[1,128,5120]{2,1,0:T(8,128)(2,1)S(1)}, bf16[1,128,5120]{2,1,0:T(8,128)(2,1)}, u32[]{:S(2)}) copy-start(bf16[1,128,5120]{2,1,0:T(8,128)(2,1)} %param.16) | copy-start | bytes 3932164
  7.2 13.6 %copy-start.11 = (bf16[1,128,256]{2,1,0:T(8,128)(2,1)S(1)}, bf16[1,128,256]{2,1,0:T(8,128)(2,1)}, u32[]{:S(2)}) copy-start(bf16[1,128,256]{2,1,0:T(8,128)(2,1)} %param.17) | copy-start | bytes 196612
  7.2 13.6 %copy-start.18 = (f32[5376]{0:T(1024)S(1)}, f32[5376]{0:T(1024)}, u32[]{:S(2)}) copy-start(f32[5376]{0:T(1024)} %param.21) | copy-start | bytes 64516
  8.3 10.8 %collective-permute-start = (bf16[3,5376]{1,0:T(4,128)(2,1)S(1)}, bf16[3,5376]{1,0:T(4,128)(2,1)S(1)}, u32[]{:S(2)}, u32[]{:S(2)}) collective-permute-start(bf16[3,5376]{1,0:T(4,128)(2,1)S(1)} %fusion.75), channel_id=1, source_target_pairs={{0,4},{4,8},{8,12},{12,16},{16,20},{20,24},{24,28},{1,5},{5,9},{9,... | collective-permute-start | bytes 96776 | tf_op jit(solution)/shard_map/ppermute | solution.py:13
  14.5 10.1 %all-to-all-start = ((bf16[128,4,20]{0,2,1:T(8,128)(2,1)}), bf16[128,4,20]{0,2,1:T(8,128)(2,1)S(1)}, u32[]{:S(2)}, u32[]{:S(2)}) async-start(bf16[128,4,20]{0,2,1:T(8,128)(2,1)} %all_to_all.30), calls=%async_computation | async-start | bytes 49152 | tf_op jit(solution)/shard_map/all_to_all | solution.py:122
  23.1 5.7 %copy-start.21 = (f32[20]{0:T(128)S(1)}, f32[20]{0:T(128)}, u32[]{:S(2)}) copy-start(f32[20]{0:T(128)} %param.23) | copy-start | bytes 244
  23.1 6.4 %copy-start.20 = (f32[20]{0:T(128)S(1)}, f32[20]{0:T(128)}, u32[]{:S(2)}) copy-start(f32[20]{0:T(128)} %param.22) | copy-start | bytes 244
  24.6 26.3 %all-to-all-start.1 = ((bf16[128,4,1280]{0,2,1:T(8,128)(2,1)}), bf16[128,4,1280]{0,2,1:T(8,128)(2,1)S(1)}, u32[]{:S(2)}, u32[]{:S(2)}) async-start(bf16[128,4,1280]{0,2,1:T(8,128)(2,1)} %bitcast.3), calls=%async_computation.1 | async-start | bytes 2621440 | tf_op jit(solution)/shard_map/all_to_all | solution.py:118
  28.7 163.0 %all-gather.7.cloned.1.call-start = ((), (), s32[]{:S(2)}) async-start(), calls=%async_computation.8 | async-start | bytes 1966080 | tf_op jit(solution)/shard_map/all_gather | solution.py:18
  63.0 9.1 %copy-start.7 = (f32[1,256,20]{1,2,0:T(8,128)}, f32[1,256,20]{1,2,0:T(8,128)S(1)}, u32[]{:S(2)}) copy-start(f32[1,256,20]{1,2,0:T(8,128)S(1)} %copy.123) | copy-start | bytes 61444 | tf_op jit(solution)/shard_map/while
  109.5 9.1 %copy-start.7 = (f32[1,256,20]{1,2,0:T(8,128)}, f32[1,256,20]{1,2,0:T(8,128)S(1)}, u32[]{:S(2)}) copy-start(f32[1,256,20]{1,2,0:T(8,128)S(1)} %copy.123) | copy-start | bytes 61444 | tf_op jit(solution)/shard_map/while
  153.5 138.1 %all-gather.5.cloned.1.call-start = ((), (), s32[]{:S(2)}) async-start(), calls=%async_computation.4 | async-start | bytes 8192000 | tf_op jit(solution)/shard_map/all_gather | solution.py:154
  154.8 5.1 %copy-start.23 = (u32[32]{0:T(128)S(1)}, u32[32]{0:T(128)}, u32[]{:S(2)}) copy-start(u32[32]{0:T(128)} %constant.76) | copy-start | bytes 388
  154.8 6.3 %copy-start.13 = (f32[4,128,20]{1,2,0:T(8,128)S(1)}, f32[4,128,20]{1,2,0:T(8,128)}, u32[]{:S(2)}) copy-start(f32[4,128,20]{1,2,0:T(8,128)} %copy-done.12) | copy-start | bytes 122884
  154.8 8.9 %copy-start.16 = (bf16[128,4,20]{0,2,1:T(8,128)(2,1)S(1)}, bf16[128,4,20]{0,2,1:T(8,128)(2,1)}, u32[]{:S(2)}) copy-start(bf16[128,4,20]{0,2,1:T(8,128)(2,1)} %copy-done.15) | copy-start | bytes 61444
  156.2 17.3 %all-to-all-start.2 = ((bf16[128,4,1280]{0,2,1:T(8,128)(2,1)}), bf16[128,4,1280]{0,2,1:T(8,128)(2,1)S(1)}, u32[]{:S(2)}, u32[]{:S(2)}) async-start(bf16[128,4,1280]{0,2,1:T(8,128)(2,1)} %bitcast.12), calls=%async_computation.2 | async-start | bytes 2621440 | tf_op jit(solution)/shard_map/all_to_all | solution.py:121
  159.8 175.1 %all-reduce.8.cloned.1.call-start = ((), (), s32[]{:S(2)}) async-start(), calls=%async_computation.7 | async-start | bytes 163840 | tf_op jit(solution)/shard_map/psum | solution.py:200
  186.8 4.9 %copy-start.6 = (f32[512,20,64]{0,2,1:T(8,128)S(1)}, f32[512,20,64]{0,2,1:T(8,128)}, u32[]{:S(2)}) copy-start(f32[512,20,64]{0,2,1:T(8,128)} %reshape.166) | copy-start | bytes 7864324
  186.8 4.9 %copy-start.10 = (bf16[512,256]{1,0:T(8,128)(2,1)S(1)}, bf16[512,256]{1,0:T(8,128)(2,1)}, u32[]{:S(2)}) copy-start(bf16[512,256]{1,0:T(8,128)(2,1)} %copy-done.9) | copy-start | bytes 786436
  186.8 4.9 %copy-start.22 = (f32[20]{0:T(128)S(1)}, f32[20]{0:T(128)}, u32[]{:S(2)}) copy-start(f32[20]{0:T(128)} %param.24) | copy-start | bytes 244
  201.5 18.9 %copy-start.14 = (bf16[16,2560]{1,0:T(8,128)(2,1)S(1)}, bf16[16,2560]{1,0:T(8,128)(2,1)}, u32[]{:S(2)}) copy-start(bf16[16,2560]{1,0:T(8,128)(2,1)} %param.28) | copy-start | bytes 245764
  280.6 108.3 %all-reduce.6.cloned.1.call-start = ((), (), s32[]{:S(2)}) async-start(), calls=%async_computation.6 | async-start | bytes 163840 | tf_op jit(solution)/shard_map/psum | solution.py:199
  281.9 153.3 %reduce-scatter.2.cloned.1.call-start = ((), (), s32[]{:S(2)}) async-start(), calls=%async_computation.5 | async-start | bytes 3276800 | tf_op jit(solution)/shard_map/reduce_scatter | solution.py:174
  (10 other events, 26.0 us)
Sparse Core Ops, SparseCore 0:
  153.6 9.6 all-gather.6
  164.9 126.6 all-gather.4
  295.1 39.6 all-reduce.7
  337.6 51.2 all-reduce.5
  392.3 42.9 reduce-scatter.1
where the time goes:
time: 448 us; the launch traced here: 443 us
  waiting for transfers between devices  151 us (34%)
  local copies, waits for them, and re-layouts  105 us (23%)
  blocking collectives  96.8 us (22%)
  matrix products  41.7 us (9%)
  other arithmetic  17.6 us (4%)
  starting transfers between devices  16 us (4%)
  between operations  14.8 us (3%)
    dynamic_update_slice x4, local copies, waits for them, and re-layouts, ssd_blocks(): lax.scan(advance, start_state, (x_heads.reshape(blocks, block_len, head_c...  56.8 us
    psum x1, waiting for transfers between devices, shards(): lax.psum((grad_a_local, grad_b_local), ('context', 'fsdp'))  52.5 us
    psum x1, blocking collectives, shards(): lax.psum((grad_a_local, grad_b_local), ('context', 'fsdp'))  51.7 us
    reduce_scatter x1, waiting for transfers between devices, shards(): lax.psum_scatter((row_slice(scale_all, start_row, lax.axis_size('tensor')...  46.4 us
    psum x1, waiting for transfers between devices, shards(): lax.psum(grad_b_part.astype(jnp.bfloat16), 'tensor').astype(jnp.float32)  35.1 us
    all_gather x1, blocking collectives, shards(): lax.all_gather(convolved[:, inner_width:], 'tensor', axis=0, tiled=True)  19.2 us
    psum x1, blocking collectives, shards(): lax.psum(adapter_piece.astype(jnp.bfloat16), 'tensor').astype(jnp.float32)  15.3 us
    dot_general x2, matrix products, advance(): jnp.einsum('hij,jhp->ihp', decay_mat * gram_mat[None], x_scaled, precisio...  11.9 us
  transfers between devices with their start and end apart: 9, of which 5 were waited for; matrix products, arithmetic and copies ran while one was open for 13% of the time, Pallas kernels for 0%

commit v1 on v0

--- a/solution.py
+++ b/solution.py
@@ -5,6 +5,12 @@
 from jax.sharding import PartitionSpec as P
 
 epsilon = 1e-05
+
+
+def summed_here(x, axis):
+    terms = lax.all_gather(x, axis, axis=0, tiled=False)
+    total = terms.sum(axis=0)
+    return total
 
 
 def passed_along(value, axis, steps):
@@ -197,7 +203,7 @@
     adapter_span = lax.all_gather(adapter_gradient, "tensor", axis=0, tiled=True)
     grad_a_local = jnp.dot(gated_output.astype(jnp.float32).T, adapter_span, precision=highest)
     grad_a, grad_b_part = lax.psum((grad_a_local, grad_b_local), ("context", "fsdp"))
-    grad_b = lax.psum(grad_b_part.astype(jnp.bfloat16), "tensor").astype(jnp.float32)
+    grad_b = summed_here(grad_b_part.astype(jnp.bfloat16), "tensor").astype(jnp.float32)
     return (summed[None], grad_a, grad_b)
 
 

time: 448 us -> 397 us (0.89)
  waiting for transfers between devices: 151 us -> 114 us
  blocking collectives: 96.8 us -> 84.1 us
    psum x1, waiting for transfers between devices: 52.5 us -> 3.88 us  [shards(): lax.psum((grad_a_local, grad_b_local), ('context', 'fsdp'))]
    all_gather x1, waiting for transfers between devices: 9.67 us -> 55.9 us  [shards(): columns = lax.all_gather(output_weight, 'fsdp', axis=1, tiled=True)]
    psum x1 -> x0, waiting for transfers between devices: 35.1 us -> none  [shards(): lax.psum(grad_b_part.astype(jnp.bfloat16), 'tensor').astype(jnp.float32)]
    psum x1, blocking collectives: 51.7 us -> 28.9 us  [shards(): lax.psum((grad_a_local, grad_b_local), ('context', 'fsdp'))]
    all_gather x0 -> x1, blocking collectives: none -> 10.2 us  [summed_here(): terms = lax.all_gather(x, axis, axis=0, tiled=False)]
  transfers between devices with their start and end apart: 9 -> 8, of which waited for: 5 -> 4; matrix products, arithmetic and copies ran while one was open for 13% -> 14% of each run, Pallas kernels for 0% -> 0%
where the time goes in v1:
time: 397 us; the launch traced here: 392 us
  waiting for transfers between devices  114 us (29%)
  local copies, waits for them, and re-layouts  105 us (26%)
  blocking collectives  84.1 us (21%)
  matrix products  41.7 us (11%)
  other arithmetic  16.7 us (4%)
  starting transfers between devices  16 us (4%)
  between operations  14.8 us (4%)
    dynamic_update_slice x4, local copies, waits for them, and re-layouts, ssd_blocks(): lax.scan(advance, start_state, (x_heads.reshape(blocks, block_len, head_c...  56.8 us
    all_gather x1, waiting for transfers between devices, shards(): columns = lax.all_gather(output_weight, 'fsdp', axis=1, tiled=True)  55.9 us
    reduce_scatter x1, waiting for transfers between devices, shards(): lax.psum_scatter((row_slice(scale_all, start_row, lax.axis_size('tensor')...  46.4 us
    psum x1, blocking collectives, shards(): lax.psum((grad_a_local, grad_b_local), ('context', 'fsdp'))  28.9 us
    all_gather x1, blocking collectives, shards(): lax.all_gather(convolved[:, inner_width:], 'tensor', axis=0, tiled=True)  19.2 us
    psum x1, blocking collectives, shards(): lax.psum(adapter_piece.astype(jnp.bfloat16), 'tensor').astype(jnp.float32)  15.3 us
    dot_general x2, matrix products, advance(): jnp.einsum('hij,jhp->ihp', decay_mat * gram_mat[None], x_scaled, precisio...  11.9 us
    convert_element_type x3, local copies, waits for them, and re-layouts, shards(): x_heads_raw.astype(jnp.float32).reshape(span_rows, local_heads, head_size)  10.9 us
  transfers between devices with their start and end apart: 8, of which 4 were waited for; matrix products, arithmetic and copies ran while one was open for 14% of the time, Pallas kernels for 0%

profile of v1, /device:TPU:0, one launch (start us, length us, event | category | flops | bytes accessed | tf_op | source)
XLA Modules:
  0.0 392.3 jit_solution(17924060496503463533)
XLA Ops:
  8.3 4.9 %collective-permute-start = (bf16[3,5376]{1,0:T(4,128)(2,1)S(1)}, bf16[3,5376]{1,0:T(4,128)(2,1)S(1)}, u32[]{:S(2)}, u32[]{:S(2)}) collective-permute-start(bf16[3,5376]{1,0:T(4,128)(2,1)S(1)} %fusion.75), channel_id=1, source_target_pairs={{0,4},{4,8},{8,12},{12,16},{16,20},{20,24},{24,28},{1,5},{5,9},{9,... | collective-permute-start | bytes 96776 | tf_op jit(solution)/shard_map/ppermute | solution.py:19
  24.6 4.2 %all-to-all-start.1 = ((bf16[128,4,1280]{0,2,1:T(8,128)(2,1)}), bf16[128,4,1280]{0,2,1:T(8,128)(2,1)S(1)}, u32[]{:S(2)}, u32[]{:S(2)}) async-start(bf16[128,4,1280]{0,2,1:T(8,128)(2,1)} %bitcast.3), calls=%async_computation.1 | async-start | bytes 2621440 | tf_op jit(solution)/shard_map/all_to_all | solution.py:124
  30.3 19.2 %all_gather.27 = bf16[512,256]{1,0:T(8,128)(2,1)S(1)} all-gather(bf16[128,256]{1,0:T(8,128)(2,1)S(1)} %slice.84), channel_id=1, replica_groups=mesh['context'=2,'tensor'=4,'fsdp'=4] {'tensor'}, dimensions={0}, use_global_device_ids=true | all-gather | bytes 327680 | tf_op jit(solution)/shard_map/all_gather | solution.py:130
  51.1 5.4 %copy.68 = f32[4,128,1280]{1,0,2:T(4,128)S(1)} copy(f32[4,128,1280]{1,2,0:T(8,128)S(1)} %convert_bitcast_fusion.1) | data formatting | bytes 5242880 | tf_op jit(solution)/shard_map/convert_element_type | solution.py:135
  59.9 93.5 %while.4 = (s32[]{:T(128)}, f32[20,64,128]{2,1,0:T(8,128)}, f32[2,256,20,64]{1,0,3,2:T(2,128)}, f32[2,256,20]{1,0,2:T(2,128)}, f32[2,256,20,64]{1,0,3,2:T(2,128)...) while((s32[]{:T(128)}, f32[20,64,128]{2,1,0:T(8,128)}, ...), condition=%wide.region_3.4_spmd.clone.clone, body=%wide.region_0.3_spmd.clone.clone.sunk | while | flops 2122191872 | bytes 18280176 | solution.py:77
  66.2 6.0 %fusion.115 = f32[256,20,64]{0,2,1:T(8,128)S(1)} fusion(f32[256,256]{1,0:T(8,128)S(1)} %fusion.114, f32[20,256]{1,0:T(8,128)S(1)} %bitcast.177, pred[256,256]{1,0:T(8,128)(4,1)S(1)} %iota_compare_fusion.2, f32[1,256,20,64]{1,0,3,2:T(1,128)S(1)} %constant_dynamic-slice_fusion.5, f32[256,20]{0,1:T(8,128)S(1)} %bitcast.181), kind=kOutput, calls=%fused_computation.15.clone.1 | convolution fusion | flops 1012203520 | bytes 2990080 | tf_op jit(solution)/shard_map/while/body/eval_jaxpr/hij,jhp->ihp/dot_general | solution.py:64
  76.5 27.0 %dynamic_update_slice.7 = f32[2,256,20,64]{1,0,3,2:T(2,128)} dynamic-update-slice(f32[2,256,20,64]{1,0,3,2:T(2,128)} %get-tuple-element.267, f32[1,256,20,64]{1,0,3,2:T(1,128)S(1)} %copy.124, s32[]{:T(128)} %get-tuple-element.265, s32[]{:T(128)} %constant.43.clone.1..sunk, s32[]{:T(128)} %constant.43.clone.1..sunk, s32[]{:T(128)} %constant.43.clone.1..sunk) | dynamic-update-slice | bytes 2621444 | tf_op jit(solution)/shard_map/while/body/jit(dynamic_update_index_in_dim)/dynamic_update_slice | solution.py:77
  112.7 6.0 %fusion.115 = f32[256,20,64]{0,2,1:T(8,128)S(1)} fusion(f32[256,256]{1,0:T(8,128)S(1)} %fusion.114, f32[20,256]{1,0:T(8,128)S(1)} %bitcast.177, pred[256,256]{1,0:T(8,128)(4,1)S(1)} %iota_compare_fusion.2, f32[1,256,20,64]{1,0,3,2:T(1,128)S(1)} %constant_dynamic-slice_fusion.5, f32[256,20]{0,1:T(8,128)S(1)} %bitcast.181), kind=kOutput, calls=%fused_computation.15.clone.1 | convolution fusion | flops 1012203520 | bytes 2990080 | tf_op jit(solution)/shard_map/while/body/eval_jaxpr/hij,jhp->ihp/dot_general | solution.py:64
  123.3 27.0 %dynamic_update_slice.7 = f32[2,256,20,64]{1,0,3,2:T(2,128)} dynamic-update-slice(f32[2,256,20,64]{1,0,3,2:T(2,128)} %get-tuple-element.267, f32[1,256,20,64]{1,0,3,2:T(1,128)S(1)} %copy.124, s32[]{:T(128)} %get-tuple-element.265, s32[]{:T(128)} %constant.43.clone.1..sunk, s32[]{:T(128)} %constant.43.clone.1..sunk, s32[]{:T(128)} %constant.43.clone.1..sunk) | dynamic-update-slice | bytes 2621444 | tf_op jit(solution)/shard_map/while/body/jit(dynamic_update_index_in_dim)/dynamic_update_slice | solution.py:77
  156.2 3.5 all-to-all-start.2
  166.6 6.9 %all-to-all-done.2 = bf16[128,4,1280]{0,2,1:T(8,128)(2,1)S(1)} async-done(((bf16[128,4,1280]{0,2,1:T(8,128)(2,1)}), bf16[128,4,1280]{0,2,1:T(8,128)(2,1)S(1)}, u32[]{:S(2)}, u32[]{:S(2)}) %all-to-all-start.2) | async-done | bytes 1310752 | tf_op jit(solution)/shard_map/all_to_all | solution.py:127
  176.1 4.3 %copy.79 = f32[4,128,1280]{1,0,2:T(4,128)} copy(f32[4,128,1280]{2,1,0:T(8,128)} %convert_bitcast_fusion) | data formatting | bytes 5242880 | tf_op jit(solution)/shard_map/convert_element_type | solution.py:155
  180.4 4.3 %reshape.166 = f32[512,20,64]{0,2,1:T(8,128)} reshape(f32[4,128,1280]{1,0,2:T(4,128)} %copy.79) | data formatting | bytes 5242880 | tf_op jit(solution)/shard_map/convert_element_type | solution.py:155
  186.8 4.9 %reshape.152 = f32[512,20,64]{0,2,1:T(8,128)} reshape(f32[2,256,20,64]{1,0,3,2:T(2,128)} %get-tuple-element.72) | data formatting | bytes 5242880 | tf_op jit(solution)/shard_map/reshape | solution.py:88
  191.8 6.3 %multiply_reduce_fusion = (bf16[512]{0:T(512)(128)(2,1)S(1)}, f32[512,20,64]{0,2,1:T(8,128)}) fusion(f32[512,20,64]{0,2,1:T(8,128)S(1)} %copy-done.6, f32[512,20,64]{0,2,1:T(8,128)} %reshape.165, f32[20]{0:T(128)S(1)} %copy-done.22, f32[512,20,64]{0,2,1:T(8,128)} %reshape.152, f32[40,64,128]{2,1,0:T(8,128)} %all-gather.8.cloned.1.call-done, ...), kind=kOutput, calls=%fused_computation.66 | convolution fusion | flops 1014169088 | bytes 11323393 | tf_op jit(solution)/shard_map/tn,hpn->thp/dot_general | solution.py:151
  198.1 3.4 copy.80
  204.7 15.3 %all-reduce.1 = (bf16[512,16]{0,1:T(8,128)(2,1)S(1)}, bf16[512]{0:T(512)(128)(2,1)S(1)}) all-reduce(bf16[512,16]{0,1:T(8,128)(2,1)S(1)} %convolution_convert_fusion, bf16[512]{0:T(512)(128)(2,1)S(1)} %get-tuple-element.195), channel_id=1, replica_groups=mesh['context'=2,'tensor'=4,'fsdp'=4] {'tensor'}, use_global_device_ids=true, to_apply=%region_9.10 | all-reduce | flops 8704 | bytes 34816 | tf_op jit(solution)/shard_map/psum | solution.py:164
  220.3 8.2 %all_gather.33 = f32[512,16]{0,1:T(8,128)S(1)} all-gather(f32[128,16]{0,1:T(8,128)S(1)} %convolution_multiply_fusion.1), channel_id=1, replica_groups=mesh['context'=2,'tensor'=4,'fsdp'=4] {'tensor'}, dimensions={0}, use_global_device_ids=true | all-gather | bytes 40960 | tf_op jit(solution)/shard_map/all_gather | solution.py:203
  229.8 55.9 %all-gather.6.cloned.1.call-done = bf16[1280,2560]{1,0:T(8,128)(2,1)} async-done(((bf16[1280,640]{1,0:T(8,128)(2,1)}), bf16[1280,2560]{1,0:T(8,128)(2,1)}) %all-gather.6.cloned.1.call-update) | async-done | bytes 6553616 | tf_op jit(solution)/shard_map/all_gather | solution.py:160
  285.7 5.7 %fusion.84 = f32[512,2560]{1,0:T(8,128)S(1)} fusion(bf16[512,1280]{1,0:T(8,128)(2,1)S(1)} %fusion.52, bf16[1280,2560]{1,0:T(8,128)(2,1)} %all-gather.6.cloned.1.call-done), kind=kOutput, calls=%fused_computation.121 | convolution fusion | flops 3355443200 | bytes 13107200 | tf_op jit(solution)/shard_map/dot_general | solution.py:170
  294.2 28.9 %all-reduce.6 = bf16[16,2560]{1,0:T(8,128)(2,1)S(1)} all-reduce(f32[16,2560]{1,0:T(8,128)S(1)} %fusion.55), channel_id=1, replica_groups=mesh['context'=2,'tensor'=4,'fsdp'=4] {'context','fsdp'}, use_global_device_ids=true, to_apply=%region_12.13 | all-reduce | flops 40960 | bytes 245760 | tf_op jit(solution)/shard_map/psum | solution.py:205
  323.1 10.2 %all-gather.2 = bf16[64,2560]{1,0:T(8,128)(2,1)S(1)} all-gather(bf16[16,2560]{1,0:T(8,128)(2,1)S(1)} %all-reduce.6), channel_id=4, replica_groups=mesh['context'=2,'tensor'=4,'fsdp'=4] {'tensor'}, dimensions={0}, use_global_device_ids=true | all-gather | bytes 409600 | tf_op jit(solution)/shard_map/all_gather | solution.py:11
  334.0 3.9 all-reduce.5.cloned.1.call-done
  337.9 46.4 %reduce-scatter.2.cloned.1.call-done = bf16[128,2560]{1,0:T(8,128)(2,1)} async-done(((bf16[512,2560]{1,0:T(8,128)(2,1)}), bf16[128,2560]{1,0:T(8,128)(2,1)}) %reduce-scatter.2.cloned.1.call-update) | async-done | bytes 655376 | tf_op jit(solution)/shard_map/reduce_scatter | solution.py:180
  (162 shorter events, 69.6 us)
Async XLA Ops:
  7.2 212.8 %copy-start = (bf16[1,128,2560]{2,1,0:T(8,128)(2,1)S(1)}, bf16[1,128,2560]{2,1,0:T(8,128)(2,1)}, u32[]{:S(2)}) copy-start(bf16[1,128,2560]{2,1,0:T(8,128)(2,1)} %param.29) | copy-start | bytes 1966084
  7.2 13.6 %copy-start.5 = (bf16[1,128,5120]{2,1,0:T(8,128)(2,1)S(1)}, bf16[1,128,5120]{2,1,0:T(8,128)(2,1)}, u32[]{:S(2)}) copy-start(bf16[1,128,5120]{2,1,0:T(8,128)(2,1)} %param.16) | copy-start | bytes 3932164
  7.2 13.6 %copy-start.11 = (bf16[1,128,256]{2,1,0:T(8,128)(2,1)S(1)}, bf16[1,128,256]{2,1,0:T(8,128)(2,1)}, u32[]{:S(2)}) copy-start(bf16[1,128,256]{2,1,0:T(8,128)(2,1)} %param.17) | copy-start | bytes 196612
  7.2 13.6 %copy-start.18 = (f32[5376]{0:T(1024)S(1)}, f32[5376]{0:T(1024)}, u32[]{:S(2)}) copy-start(f32[5376]{0:T(1024)} %param.21) | copy-start | bytes 64516
  8.3 10.8 %collective-permute-start = (bf16[3,5376]{1,0:T(4,128)(2,1)S(1)}, bf16[3,5376]{1,0:T(4,128)(2,1)S(1)}, u32[]{:S(2)}, u32[]{:S(2)}) collective-permute-start(bf16[3,5376]{1,0:T(4,128)(2,1)S(1)} %fusion.75), channel_id=1, source_target_pairs={{0,4},{4,8},{8,12},{12,16},{16,20},{20,24},{24,28},{1,5},{5,9},{9,... | collective-permute-start | bytes 96776 | tf_op jit(solution)/shard_map/ppermute | solution.py:19
  14.5 10.1 %all-to-all-start = ((bf16[128,4,20]{0,2,1:T(8,128)(2,1)}), bf16[128,4,20]{0,2,1:T(8,128)(2,1)S(1)}, u32[]{:S(2)}, u32[]{:S(2)}) async-start(bf16[128,4,20]{0,2,1:T(8,128)(2,1)} %all_to_all.30), calls=%async_computation | async-start | bytes 49152 | tf_op jit(solution)/shard_map/all_to_all | solution.py:128
  23.1 5.7 %copy-start.21 = (f32[20]{0:T(128)S(1)}, f32[20]{0:T(128)}, u32[]{:S(2)}) copy-start(f32[20]{0:T(128)} %param.23) | copy-start | bytes 244
  23.1 6.4 %copy-start.20 = (f32[20]{0:T(128)S(1)}, f32[20]{0:T(128)}, u32[]{:S(2)}) copy-start(f32[20]{0:T(128)} %param.22) | copy-start | bytes 244
  24.6 26.3 %all-to-all-start.1 = ((bf16[128,4,1280]{0,2,1:T(8,128)(2,1)}), bf16[128,4,1280]{0,2,1:T(8,128)(2,1)S(1)}, u32[]{:S(2)}, u32[]{:S(2)}) async-start(bf16[128,4,1280]{0,2,1:T(8,128)(2,1)} %bitcast.3), calls=%async_computation.1 | async-start | bytes 2621440 | tf_op jit(solution)/shard_map/all_to_all | solution.py:124
  28.7 163.0 %all-gather.8.cloned.1.call-start = ((), (), s32[]{:S(2)}) async-start(), calls=%async_computation.7 | async-start | bytes 1966080 | tf_op jit(solution)/shard_map/all_gather | solution.py:24
  63.0 9.1 %copy-start.7 = (f32[1,256,20]{1,2,0:T(8,128)}, f32[1,256,20]{1,2,0:T(8,128)S(1)}, u32[]{:S(2)}) copy-start(f32[1,256,20]{1,2,0:T(8,128)S(1)} %copy.123) | copy-start | bytes 61444 | tf_op jit(solution)/shard_map/while
  109.5 9.1 %copy-start.7 = (f32[1,256,20]{1,2,0:T(8,128)}, f32[1,256,20]{1,2,0:T(8,128)S(1)}, u32[]{:S(2)}) copy-start(f32[1,256,20]{1,2,0:T(8,128)S(1)} %copy.123) | copy-start | bytes 61444 | tf_op jit(solution)/shard_map/while
  153.5 132.2 %all-gather.6.cloned.1.call-start = ((), (), s32[]{:S(2)}) async-start(), calls=%async_computation.4 | async-start | bytes 8192000 | tf_op jit(solution)/shard_map/all_gather | solution.py:160
  154.8 5.1 %copy-start.23 = (u32[32]{0:T(128)S(1)}, u32[32]{0:T(128)}, u32[]{:S(2)}) copy-start(u32[32]{0:T(128)} %constant.78) | copy-start | bytes 388
  154.8 6.3 %copy-start.13 = (f32[4,128,20]{1,2,0:T(8,128)S(1)}, f32[4,128,20]{1,2,0:T(8,128)}, u32[]{:S(2)}) copy-start(f32[4,128,20]{1,2,0:T(8,128)} %copy-done.12) | copy-start | bytes 122884
  154.8 8.9 %copy-start.16 = (bf16[128,4,20]{0,2,1:T(8,128)(2,1)S(1)}, bf16[128,4,20]{0,2,1:T(8,128)(2,1)}, u32[]{:S(2)}) copy-start(bf16[128,4,20]{0,2,1:T(8,128)(2,1)} %copy-done.15) | copy-start | bytes 61444
  156.2 17.3 %all-to-all-start.2 = ((bf16[128,4,1280]{0,2,1:T(8,128)(2,1)}), bf16[128,4,1280]{0,2,1:T(8,128)(2,1)S(1)}, u32[]{:S(2)}, u32[]{:S(2)}) async-start(bf16[128,4,1280]{0,2,1:T(8,128)(2,1)} %bitcast.12), calls=%async_computation.2 | async-start | bytes 2621440 | tf_op jit(solution)/shard_map/all_to_all | solution.py:127
  159.8 178.1 %all-reduce.5.cloned.1.call-start = ((), (), s32[]{:S(2)}) async-start(), calls=%async_computation.6 | async-start | bytes 163840 | tf_op jit(solution)/shard_map/psum | solution.py:205
  180.4 4.3 %copy-start.2 = (f32[4,128,1280]{1,0,2:T(4,128)S(1)}, f32[4,128,1280]{1,0,2:T(4,128)}, u32[]{:S(2)}) copy-start(f32[4,128,1280]{1,0,2:T(4,128)} %copy-done.1) | copy-start | bytes 7864324
  186.8 4.9 %copy-start.6 = (f32[512,20,64]{0,2,1:T(8,128)S(1)}, f32[512,20,64]{0,2,1:T(8,128)}, u32[]{:S(2)}) copy-start(f32[512,20,64]{0,2,1:T(8,128)} %reshape.166) | copy-start | bytes 7864324
  186.8 4.9 %copy-start.10 = (bf16[512,256]{1,0:T(8,128)(2,1)S(1)}, bf16[512,256]{1,0:T(8,128)(2,1)}, u32[]{:S(2)}) copy-start(bf16[512,256]{1,0:T(8,128)(2,1)} %copy-done.9) | copy-start | bytes 786436
  186.8 4.9 %copy-start.22 = (f32[20]{0:T(128)S(1)}, f32[20]{0:T(128)}, u32[]{:S(2)}) copy-start(f32[20]{0:T(128)} %param.24) | copy-start | bytes 244
  201.5 18.5 %copy-start.14 = (bf16[16,2560]{1,0:T(8,128)(2,1)S(1)}, bf16[16,2560]{1,0:T(8,128)(2,1)}, u32[]{:S(2)}) copy-start(bf16[16,2560]{1,0:T(8,128)(2,1)} %param.28) | copy-start | bytes 245764
  229.7 154.6 %reduce-scatter.2.cloned.1.call-start = ((), (), s32[]{:S(2)}) async-start(), calls=%async_computation.5 | async-start | bytes 3276800 | tf_op jit(solution)/shard_map/reduce_scatter | solution.py:180
  (9 other events, 21.8 us)
Sparse Core Ops, SparseCore 0:
  153.6 9.6 all-gather.7
  164.9 120.7 all-gather.5
  288.6 49.2 all-reduce.4
  341.3 42.9 reduce-scatter.1
